TPU v7x, 32 devices: a 4x4x1 block of a 4x4x8 slice. The times are simulated.
32 devices in a mesh: data: 1 (over z), ffn: 4 (over y), hid: 8 (over x, core).
Axes of the slice: x: 4, y: 4, z: 1, core: 2. Of those that a mesh axis runs over, the one named last changes fastest.
The devices are a block of a 4x4x8 slice.
Arguments:
- x_in: bfloat16 [64, 4096], P('data', 'hid')
- gain_one: float32 [4096], P('hid')
- gain_two: float32 [4096], P('hid')
- w_gate: bfloat16 [4096, 11008], P('hid', 'ffn')
- w_up: bfloat16 [4096, 11008], P('hid', 'ffn')
- w_down: bfloat16 [11008, 4096], P('ffn', 'hid')
- w_qkv: bfloat16 [4096, 12288], P('hid', 'ffn')
- dx_out: bfloat16 [64, 4096], P('data', 'hid')
- d_qkv: bfloat16 [64, 12288], P('data', 'ffn')
Outputs:
- output 1: bfloat16 [64, 4096], P('data', 'hid')
- output 2: bfloat16 [4096, 11008], P(('data', 'hid'), 'ffn')
- output 3: bfloat16 [4096, 11008], P(('data', 'hid'), 'ffn')
- output 4: bfloat16 [11008, 4096], P(('data', 'ffn'), 'hid')
- output 5: bfloat16 [4096, 12288], P(('data', 'hid'), 'ffn')
- output 6: float32 [4096], P(('data', 'hid'))
- output 7: float32 [4096], P(('data', 'hid'))
All inputs are finite; a program needn't handle non-finite values.
Results may differ from a plain program's by a relative error of at most 0.00556686.
Values are sent between devices in bfloat16 or wider.
A program may use at most 768 MiB of HBM per device.

v0:
```python
import jax
import jax.numpy as jnp
from jax import lax
from jax.sharding import PartitionSpec as P

NORM_EPS = 1e-6


def dot_nt(a_mat, b_mat):
    return lax.dot_general(a_mat, b_mat, (((1,), (1,)), ((), ())), preferred_element_type=jnp.float32)


def dot_tn(a_mat, b_mat):
    return lax.dot_general(a_mat, b_mat, (((0,), (0,)), ((), ())), preferred_element_type=jnp.float32)


def norm_forward(z_val, gain_vec, d_model):
    sq_part = jnp.sum(z_val * z_val, axis=-1, keepdims=True)
    inv_rms = lax.rsqrt(lax.psum(sq_part, "hid") / d_model + NORM_EPS)
    return inv_rms, (z_val * inv_rms * gain_vec).astype(jnp.bfloat16)


def norm_backward(z_val, gain_vec, inv_rms, d_norm, d_model):
    g_dn = gain_vec * d_norm
    dot_tok = lax.psum(jnp.sum(g_dn * z_val, axis=-1, keepdims=True), "hid")
    d_input = inv_rms * g_dn - z_val * (inv_rms ** 3) * (dot_tok / d_model)
    d_gain = jnp.sum(d_norm * z_val * inv_rms, axis=0)
    return d_input, d_gain


def solution(mesh):
    hid_size = mesh.shape["hid"]

    def local_step(x_in, gain_one, gain_two, w_gate, w_up, w_down, w_qkv, dx_out, d_qkv):
        d_model = x_in.shape[1] * hid_size
        x_f32 = x_in.astype(jnp.float32)
        inv_one, normed_one = norm_forward(x_f32, gain_one, d_model)
        gate_part = jnp.dot(normed_one, w_gate, preferred_element_type=jnp.float32)
        up_part = jnp.dot(normed_one, w_up, preferred_element_type=jnp.float32)
        gate_pre, up_pre = lax.psum((gate_part, up_part), "hid")
        gate_silu = jax.nn.silu(gate_pre)
        act_bf = (gate_silu * up_pre).astype(jnp.bfloat16)
        down_sum = lax.psum(jnp.dot(act_bf, w_down, preferred_element_type=jnp.float32), "ffn")
        resid_f32 = (x_f32 + down_sum).astype(jnp.bfloat16).astype(jnp.float32)
        inv_two, normed_two = norm_forward(resid_f32, gain_two, d_model)
        dw_qkv = dot_tn(normed_two, d_qkv).astype(jnp.bfloat16)
        d_normed_two = lax.psum(dot_nt(d_qkv, w_qkv), "ffn")
        d_resid, d_gain_two = norm_backward(resid_f32, gain_two, inv_two, d_normed_two, d_model)
        d_res_tot = dx_out.astype(jnp.float32) + d_resid
        d_res_bf = d_res_tot.astype(jnp.bfloat16)
        dw_down = dot_tn(act_bf, d_res_bf).astype(jnp.bfloat16)
        d_act = lax.psum(dot_nt(d_res_bf, w_down), "hid")
        gate_sig = jax.nn.sigmoid(gate_pre)
        d_gate = (d_act * up_pre * gate_sig * (1.0 + gate_pre * (1.0 - gate_sig))).astype(jnp.bfloat16)
        d_up = (d_act * gate_silu).astype(jnp.bfloat16)
        dw_gate = dot_tn(normed_one, d_gate).astype(jnp.bfloat16)
        dw_up = dot_tn(normed_one, d_up).astype(jnp.bfloat16)
        d_normed_one = lax.psum(dot_nt(d_gate, w_gate) + dot_nt(d_up, w_up), "ffn")
        d_in, d_gain_one = norm_backward(x_f32, gain_one, inv_one, d_normed_one, d_model)
        dx_in = (d_res_tot + d_in).astype(jnp.bfloat16)
        return dx_in, dw_gate, dw_up, dw_down, dw_qkv, d_gain_one, d_gain_two

    tok_spec = P("data", "hid")
    in_specs = (tok_spec, P("hid"), P("hid"), P("hid", "ffn"), P("hid", "ffn"), P("ffn", "hid"), P("hid", "ffn"), tok_spec, P("data", "ffn"))
    out_specs = (tok_spec, P(("data", "hid"), "ffn"), P(("data", "hid"), "ffn"), P(("data", "ffn"), "hid"), P(("data", "hid"), "ffn"), P(("data", "hid")), P(("data", "hid")))
    return jax.shard_map(local_step, mesh=mesh, in_specs=in_specs, out_specs=out_specs, check_vma=False)
```

profile of v0, /device:TPU:97, one launch (start us, length us, event | category | flops | bytes accessed | tf_op | source)
XLA Modules:
  0.0 283.2 jit_solution(14565739608285790841)
XLA Ops:
  7.2 0.0 copy-start
  7.2 0.0 copy-start.4
  7.2 0.0 copy-start.8
  7.2 0.1 all-reduce.11.cloned.1.call-start
  7.3 1.1 fusion.10
  8.4 13.9 %psum.70 = f32[64,1]{0,1:T(1,128)S(1)} all-reduce(f32[64,1]{0,1:T(1,128)S(1)} %bitcast.34), channel_id=1, replica_groups=mesh['data'=1,'ffn'=4,'hid'=8] {'hid'}, use_global_device_ids=true, to_apply=%region_1.0 | all-reduce | flops 64 | bytes 512 | tf_op jit(solution)/shard_map/psum | solution.py:19
  22.3 3.8 %fusion.33 = f32[64,2752]{1,0:T(8,128)} fusion(bf16[512,2752]{0,1:T(8,128)(2,1)} %param.13, bf16[64,512]{1,0:T(8,128)(2,1)} %param.9, f32[512]{0:T(512)} %param.10, f32[64]{0:T(128)S(1)} %get-tuple-element.20), kind=kOutput, calls=%fused_computation.56 | convolution fusion | flops 180486144 | bytes 3590400 | tf_op jit(solution)/shard_map/dot_general | solution.py:39
  26.1 0.0 copy-done.4
  26.1 0.0 copy-done.8
  26.1 0.0 copy-done.1
  26.1 1.9 fusion.35
  28.0 0.1 all-reduce.11.cloned.1.call-update
  28.0 0.1 all-reduce.13.cloned.1.call-start
  28.1 0.0 copy-done
  28.1 2.7 fusion.39
  30.8 56.4 %all-reduce.11.cloned.1.call-done = (f32[64,2752]{1,0:T(8,128)}, f32[64,2752]{1,0:T(8,128)}) async-done(((f32[64,2752]{1,0:T(8,128)}, f32[64,2752]{1,0:T(8,128)}), (f32[64,2752]{1,0:T(8,128)}, f32[64,2752]{1,0:T(8,128)})) %all-reduce.11.cloned.1.call-update) | async-done | bytes 1409040 | tf_op jit(solution)/shard_map/psum | solution.py:40
  87.2 1.6 multiply_convert_fusion.2
  88.8 0.0 copy-start.5
  88.8 0.7 copy-done.5
  89.5 3.1 %fusion.38 = f32[64,512]{1,0:T(8,128)} fusion(bf16[64,2752]{1,0:T(8,128)(2,1)S(1)} %multiply_convert_fusion.2, bf16[2752,512]{1,0:T(8,128)(2,1)} %param.14), kind=kOutput, calls=%fused_computation.58 | convolution fusion | flops 180355072 | bytes 3301376 | tf_op jit(solution)/shard_map/dot_general | solution.py:43
  92.6 0.1 all-reduce.13.cloned.1.call-update
  92.6 0.1 all-reduce.7.cloned.1.call-start
  92.7 36.2 %all-reduce.13.cloned.1.call-done = (f32[64,512]{1,0:T(8,128)}, f32[64,512]{1,0:T(8,128)}) async-done(((f32[64,512]{1,0:T(8,128)}, f32[64,512]{1,0:T(8,128)}), (f32[64,512]{1,0:T(8,128)}, f32[64,512]{1,0:T(8,128)})) %all-reduce.13.cloned.1.call-update) | async-done | bytes 262160 | tf_op jit(solution)/shard_map/psum | solution.py:43
  128.9 1.0 fusion.1
  129.9 14.6 %psum.74 = f32[64,1]{0,1:T(1,128)S(1)} all-reduce(f32[64,1]{0,1:T(1,128)S(1)} %bitcast.31), channel_id=1, replica_groups=mesh['data'=1,'ffn'=4,'hid'=8] {'hid'}, use_global_device_ids=true, to_apply=%region_6.7 | all-reduce | flops 64 | bytes 512 | tf_op jit(solution)/shard_map/psum | solution.py:19
  144.5 0.0 copy-done.10
  144.5 1.6 fusion.9
  146.1 12.5 %psum.76 = f32[64,1]{0,1:T(1,128)S(1)} all-reduce(f32[64,1]{0,1:T(1,128)S(1)} %bitcast.32), channel_id=1, replica_groups=mesh['data'=1,'ffn'=4,'hid'=8] {'hid'}, use_global_device_ids=true, to_apply=%region_9.10 | all-reduce | flops 64 | bytes 512 | tf_op jit(solution)/shard_map/psum | solution.py:25
  158.6 1.0 fusion.4
  159.6 3.6 %fusion.25 = f32[64,2752]{1,0:T(8,128)} fusion(bf16[2752,512]{1,0:T(8,128)(2,1)} %param.14, f32[64,512]{1,0:T(8,128)S(1)} %fusion.4), kind=kOutput, calls=%fused_computation.44 | convolution fusion | flops 180387840 | bytes 3653632 | tf_op jit(solution)/shard_map/dot_general | solution.py:10
  163.2 0.1 all-reduce.7.cloned.1.call-update
  163.3 0.1 all-reduce.9.cloned.1.call-start
  163.3 0.0 copy-start.7
  163.3 3.5 %convolution_convert_fusion.1 = bf16[2752,512]{1,0:T(8,128)(2,1)} fusion(bf16[64,2752]{1,0:T(8,128)(2,1)} %copy-done.5, f32[64,512]{1,0:T(8,128)S(1)} %fusion.4), kind=kOutput, calls=%fused_computation.1 | convolution fusion | flops 181796864 | bytes 3301376 | tf_op jit(solution)/shard_map/dot_general | solution.py:14
  166.9 2.7 convolution_convert_fusion
  169.6 46.4 %all-reduce.7.cloned.1.call-done = f32[64,2752]{1,0:T(8,128)} async-done(((f32[64,2752]{1,0:T(8,128)}), f32[64,2752]{1,0:T(8,128)}) %all-reduce.7.cloned.1.call-update) | async-done | bytes 704528 | tf_op jit(solution)/shard_map/psum | solution.py:52
  216.0 2.0 multiply_convert_fusion
  218.1 0.7 copy-done.6
  218.8 0.6 fusion.40
  219.4 0.0 copy-start.3
  219.4 2.5 convolution_convert_fusion.2
  221.9 1.3 convolution_add_fusion
  223.2 0.1 all-reduce.9.cloned.1.call-update
  223.2 3.5 %convolution_convert_fusion.3 = bf16[512,2752]{0,1:T(8,128)(2,1)} fusion(bf16[64,2752]{1,0:T(8,128)(2,1)} %copy-done.6, bf16[64,512]{1,0:T(8,128)(2,1)S(1)} %copy-done.4, f32[512]{0:T(512)S(1)} %copy-done.8, f32[64]{0:T(128)S(1)} %get-tuple-element.20), kind=kOutput, calls=%fused_computation.3 | convolution fusion | flops 181895168 | bytes 3238144 | tf_op jit(solution)/shard_map/dot_general | solution.py:14
  226.7 32.2 %all-reduce.9.cloned.1.call-done = f32[64,512]{1,0:T(8,128)} async-done(((f32[64,512]{1,0:T(8,128)}), f32[64,512]{1,0:T(8,128)}) %all-reduce.9.cloned.1.call-update) | async-done | bytes 131088 | tf_op jit(solution)/shard_map/psum | solution.py:58
  259.0 1.6 fusion.20
  260.6 14.5 %psum.79 = f32[64,1]{0,1:T(1,128)S(1)} all-reduce(f32[64,1]{0,1:T(1,128)S(1)} %bitcast.33), channel_id=1, replica_groups=mesh['data'=1,'ffn'=4,'hid'=8] {'hid'}, use_global_device_ids=true, to_apply=%region_13.14 | all-reduce | flops 64 | bytes 512 | tf_op jit(solution)/shard_map/psum | solution.py:25
  275.0 1.6 fusion.17
  (13 shorter events, 0.0 us)
Async XLA Ops:
  7.2 20.9 %copy-start = (bf16[512,3072]{1,0:T(8,128)(2,1)S(1)}, bf16[512,3072]{1,0:T(8,128)(2,1)}, u32[]{:S(2)}) copy-start(bf16[512,3072]{1,0:T(8,128)(2,1)} %param.15) | copy-start | bytes 9437188
  7.2 18.9 %copy-start.4 = (bf16[64,512]{1,0:T(8,128)(2,1)S(1)}, bf16[64,512]{1,0:T(8,128)(2,1)}, u32[]{:S(2)}) copy-start(bf16[64,512]{1,0:T(8,128)(2,1)} %param.9) | copy-start | bytes 196612
  7.2 18.9 %copy-start.8 = (f32[512]{0:T(512)S(1)}, f32[512]{0:T(512)}, u32[]{:S(2)}) copy-start(f32[512]{0:T(512)} %param.10) | copy-start | bytes 6148
  7.2 80.0 %all-reduce.11.cloned.1.call-start = ((), (), s32[]{:S(2)}) async-start(), calls=%async_computation.2 | async-start | bytes 2883584 | tf_op jit(solution)/shard_map/psum | solution.py:40
  22.3 3.9 %copy-start.1 = (bf16[512,2752]{0,1:T(8,128)(2,1)S(1)}, bf16[512,2752]{0,1:T(8,128)(2,1)}, u32[]{:S(2)}) copy-start(bf16[512,2752]{0,1:T(8,128)(2,1)} %param.12) | copy-start | bytes 8454148
  28.0 100.8 %all-reduce.13.cloned.1.call-start = ((), (), s32[]{:S(2)}) async-start(), calls=%async_computation.3 | async-start | bytes 524288 | tf_op jit(solution)/shard_map/psum | solution.py:43
  87.2 57.3 %copy-start.10 = (f32[512]{0:T(512)S(1)}, f32[512]{0:T(512)}, u32[]{:S(2)}) copy-start(f32[512]{0:T(512)} %param.11) | copy-start | bytes 6148
  87.2 71.3 %copy-start.9 = (bf16[64,512]{1,0:T(8,128)(2,1)S(1)}, bf16[64,512]{1,0:T(8,128)(2,1)}, u32[]{:S(2)}) copy-start(bf16[64,512]{1,0:T(8,128)(2,1)} %param.16) | copy-start | bytes 196612
  88.8 0.7 copy-start.5
  92.6 123.4 %all-reduce.7.cloned.1.call-start = ((), (), s32[]{:S(2)}) async-start(), calls=%async_computation | async-start | bytes 1441792 | tf_op jit(solution)/shard_map/psum | solution.py:52
  163.3 95.7 %all-reduce.9.cloned.1.call-start = ((), (), s32[]{:S(2)}) async-start(), calls=%async_computation.1 | async-start | bytes 262144 | tf_op jit(solution)/shard_map/psum | solution.py:58
  163.3 3.5 %copy-start.7 = (bf16[64,3072]{1,0:T(8,128)(2,1)S(1)}, bf16[64,3072]{1,0:T(8,128)(2,1)}, u32[]{:S(2)}) copy-start(bf16[64,3072]{1,0:T(8,128)(2,1)} %param.17) | copy-start | bytes 1179652
  216.0 2.8 copy-start.2
  218.0 0.7 copy-start.6
  219.4 2.5 copy-start.3
Sparse Core Ops, SparseCore 0:
  28.1 59.0 all-reduce.10
  92.8 36.0 all-reduce.12
  163.4 52.5 all-reduce.6
  223.4 35.5 all-reduce.8
where the time goes:
time: 284 us; the launch traced here: 283 us
  waiting for transfers between devices  171 us (60%)
  blocking collectives  55.4 us (20%)
  matrix products  29.2 us (10%)
  between operations  13.9 us (5%)
  other arithmetic  11.5 us (4%)
    psum x1, waiting for transfers between devices, local_step(): gate_pre, up_pre = lax.psum((gate_part, up_part), 'hid')  56.4 us
    psum x1, waiting for transfers between devices, local_step(): d_act = lax.psum(dot_nt(d_res_bf, w_down), 'hid')  46.4 us
    psum x1, waiting for transfers between devices, local_step(): lax.psum(jnp.dot(act_bf, w_down, preferred_element_type=jnp.float32), 'ffn')  36.2 us
    psum x1, waiting for transfers between devices, local_step(): d_normed_one = lax.psum(dot_nt(d_gate, w_gate) + dot_nt(d_up, w_up), 'ffn')  32.2 us
    psum x2, blocking collectives, norm_forward(): inv_rms = lax.rsqrt(lax.psum(sq_part, 'hid') / d_model + NORM_EPS)  28.5 us
    psum x2, blocking collectives, norm_backward(): dot_tok = lax.psum(jnp.sum(g_dn * z_val, axis=-1, keepdims=True), 'hid')  26.9 us
    dot_general x4, matrix products, dot_tn(): lax.dot_general(a_mat, b_mat, (((0,), (0,)), ((), ())), preferred_element...  12.3 us
    dot_general x4, matrix products, dot_nt(): lax.dot_general(a_mat, b_mat, (((1,), (1,)), ((), ())), preferred_element...  8.2 us
  transfers between devices with their start and end apart: 4, of which 4 were waited for; matrix products, arithmetic and copies ran while one was open for 4% of the time, Pallas kernels for 0%

commit v1 on v0

v1 whole, which is shorter than its diff:
```python
import functools

import jax
import jax.numpy as jnp
from jax import lax
from jax.experimental import pallas as pl
from jax.experimental.pallas import tpu as pltpu
from jax.sharding import PartitionSpec as P

NORM_EPS = 1e-6
F32 = jnp.float32
BF16 = jnp.bfloat16
MESH = pl.DeviceIdType.MESH
VMEM_LIMIT = 60 * 1024 * 1024
LANES = 128
CHUNK = 512


def dot_nn(a_mat, b_mat):
    return lax.dot_general(a_mat, b_mat, (((1,), (0,)), ((), ())), preferred_element_type=F32)


def dot_nt(a_mat, b_mat):
    return lax.dot_general(a_mat, b_mat, (((1,), (1,)), ((), ())), preferred_element_type=F32)


def dot_tn(a_mat, b_mat):
    return lax.dot_general(a_mat, b_mat, (((0,), (0,)), ((), ())), preferred_element_type=F32)


def half_width(width):
    return -(-width // (2 * LANES)) * LANES


def chunk_list(half):
    out, at = [], 0
    while at < half:
        size = min(CHUNK, half - at)
        out.append((at, size))
        at += size
    return out


def column_to_row(col, shift):
    tokens = col.shape[0]
    row_id = lax.broadcasted_iota(jnp.int32, (tokens, LANES), 0)
    lane_id = lax.broadcasted_iota(jnp.int32, (tokens, LANES), 1)
    return jnp.sum(jnp.where(lane_id == row_id + shift, jnp.broadcast_to(col, (tokens, LANES)), 0.0), axis=0, keepdims=True)


def row_to_column(row, tokens, shift):
    row_id = lax.broadcasted_iota(jnp.int32, (tokens, LANES), 0)
    lane_id = lax.broadcasted_iota(jnp.int32, (tokens, LANES), 1)
    return jnp.sum(jnp.where(lane_id == row_id + shift, jnp.broadcast_to(row, (tokens, LANES)), 0.0), axis=1, keepdims=True)


def chain_kernel(cfg, *refs):
    n_hid, n_ffn, tokens, width, ffw, qw = cfg["n_hid"], cfg["n_ffn"], cfg["tokens"], cfg["width"], cfg["ffw"], cfg["qw"]
    chips = n_hid // 2
    tb = tokens // chips
    half = half_width(ffw)
    chunks = chunk_list(half)
    nj = len(chunks)
    d_model = width * n_hid
    it = iter(refs)
    x_h, g1_h, g2_h, wg_h, wu_h, wd_h, wq_h, dxo_h, dq_h = [next(it) for _ in range(9)]
    dx_o, dg1_o, dg2_o, n1_o, n2_o, eb_o, a_o, dgu_o = [next(it) for _ in range(8)]
    x_v, g1_v, g2_v, wg_v, wu_v, wd_v, wq_v, dxo_v, dq_v = [next(it) for _ in range(9)]
    n1_v, n2_v, eb_v, e_v, dn2_v, stat1, stat2, stat3, dp_v, dn1_v, acc_v, dn2_s = [next(it) for _ in range(12)]
    part = [next(it) for _ in range(nj)]
    rx = [next(it) for _ in range(nj)]
    sb = [next(it) for _ in range(nj)]
    rr = [next(it) for _ in range(nj)]
    av = [next(it) for _ in range(nj)]
    sil = [next(it) for _ in range(nj)]
    pre = [next(it) for _ in range(nj)]
    part2 = [next(it) for _ in range(nj)]
    rx2 = [next(it) for _ in range(nj)]
    sb2 = [next(it) for _ in range(nj)]
    rr2 = [next(it) for _ in range(nj)]
    dgu = [next(it) for _ in range(nj)]
    load_sem, out_sem, send_sem, recv_sem, row_sem = [next(it) for _ in range(5)]

    hid = lax.axis_index("hid")
    ffn = lax.axis_index("ffn")
    chip = hid // 2
    core = hid % 2
    partner = chip * 2 + (1 - core)
    my_rows = pl.ds(pl.multiple_of(chip * tb, tb), tb)

    def hid_peer(d):
        return {"hid": (hid + d) % n_hid}

    def ffn_peer(d):
        return {"ffn": (ffn + d) % n_ffn}

    def chip_peer(d):
        return {"hid": ((chip + d) % chips) * 2 + core}

    n_sem = [0]
    sent = []

    def remote(src, dst, dev):
        s = n_sem[0]
        n_sem[0] += 1
        cp = pltpu.make_async_remote_copy(src_ref=src, dst_ref=dst, send_sem=send_sem.at[s], recv_sem=recv_sem.at[s], device_id=dev, device_id_type=MESH)
        cp.start()
        sent.append(cp)
        return cp

    loads = {}

    def load(name, src, dst):
        cp = pltpu.make_async_copy(src, dst, load_sem.at[len(loads)])
        cp.start()
        loads[name] = cp

    load("x", x_h, x_v)
    load("g1", g1_h, g1_v)
    load("dq", dq_h, dq_v)
    load("wq", wq_h, wq_v)
    load("wg", wg_h, wg_v)
    load("wu", wu_h, wu_v)
    load("wd", wd_h, wd_v.at[pl.ds(0, ffw)])
    load("g2", g2_h, g2_v)
    load("dxo", dxo_h, dxo_v)

    outs = []

    def store(src, dst):
        cp = pltpu.make_async_copy(src, dst, out_sem.at[len(outs)])
        cp.start()
        outs.append(cp)

    barrier = pltpu.get_barrier_semaphore()
    for d in range(1, n_hid):
        pl.semaphore_signal(barrier, inc=1, device_id=hid_peer(d), device_id_type=MESH)
    for d in range(1, n_ffn):
        pl.semaphore_signal(barrier, inc=1, device_id=ffn_peer(d), device_id_type=MESH)

    if 2 * half > ffw:
        wd_v[pl.ds(ffw, 2 * half - ffw), :] = jnp.zeros((2 * half - ffw, width), BF16)

    loads["x"].wait()
    x_f32 = x_v[...].astype(F32)
    stat1[pl.ds(hid, 1)] = column_to_row(jnp.sum(x_f32 * x_f32, axis=-1, keepdims=True), 0)[None]

    pl.semaphore_wait(barrier, n_hid - 1 + n_ffn - 1)
    st1 = [remote(stat1.at[hid], stat1.at[hid], hid_peer(d)) for d in range(1, n_hid)]
    for d in range(1, n_ffn):
        pl.semaphore_signal(row_sem, inc=1, device_id=ffn_peer(d), device_id_type=MESH)

    loads["dq"].wait()
    loads["wq"].wait()
    dn2_v[pl.ds(ffn, 1)] = dot_nt(dq_v[...], wq_v[...])[None]
    dn2_cp = [remote(dn2_v.at[ffn], dn2_v.at[ffn], ffn_peer(d)) for d in range(1, n_ffn)]

    loads["g1"].wait()
    for cp in st1:
        cp.wait_recv()
    ssq1 = row_to_column(jnp.sum(stat1[...], axis=0), tokens, 0)
    r1 = lax.rsqrt(ssq1 / d_model + NORM_EPS)
    n1_v[...] = (x_v[...].astype(F32) * r1 * g1_v[...]).astype(BF16)
    store(n1_v, n1_o)

    loads["wg"].wait()
    loads["wu"].wait()
    d2d = []
    for j, (c0, cw) in enumerate(chunks):
        for hf in range(2):
            lo = hf * half + c0
            valid = min(cw, ffw - lo)
            for gu, w_v in enumerate((wg_v, wu_v)):
                part[j][hf, gu, :, 0:valid] = dot_nn(n1_v[...], w_v[:, lo : lo + valid])
                if valid < cw:
                    part[j][hf, gu, :, valid:cw] = jnp.zeros((tokens, cw - valid), F32)
        d2d.append(remote(part[j].at[1 - core], rx[j], {"hid": partner}))
    rs = []
    for j, (c0, cw) in enumerate(chunks):
        d2d[j].wait_recv()
        for b in range(chips):
            rows = slice(b * tb, (b + 1) * tb)
            sb[j][b] = (part[j][core, :, rows, :] + rx[j][:, rows, :]).astype(sb[j].dtype)
        rs.append([remote(sb[j].at[(chip + d) % chips], rr[j].at[d - 1], chip_peer(d)) for d in range(1, chips)])
    ag = []
    for j, (c0, cw) in enumerate(chunks):
        for cp in rs[j]:
            cp.wait_recv()
        tot = part[j][core, :, my_rows, :] + rx[j][:, my_rows, :]
        for d in range(chips - 1):
            tot = tot + rr[j][d].astype(F32)
        gate, up = tot[0], tot[1]
        sig = jax.nn.sigmoid(gate)
        silu = gate * sig
        av[j][core, my_rows, :] = (silu * up).astype(BF16)
        ag.append([remote(av[j].at[core, my_rows], av[j].at[core, my_rows], chip_peer(d)) for d in range(1, chips)])
        sil[j][...] = silu
        pre[j][...] = up * sig * (1.0 + gate * (1.0 - sig))
    loads["wd"].wait()
    relay = []
    for j, (c0, cw) in enumerate(chunks):
        for cp in ag[j]:
            cp.wait_recv()
        relay.append(remote(av[j].at[core], av[j].at[core], {"hid": partner}))
        w_rows = pl.ds(pl.multiple_of(core * half, LANES) + c0, cw)
        prod = dot_nn(av[j][core], wd_v[w_rows, :])
        acc_v[...] = prod if j == 0 else acc_v[...] + prod
    for j, (c0, cw) in enumerate(chunks):
        relay[j].wait_recv()
        w_rows = pl.ds(pl.multiple_of((1 - core) * half, LANES) + c0, cw)
        acc_v[...] += dot_nn(av[j][1 - core], wd_v[w_rows, :])
    dp_v[pl.ds(ffn, 1)] = acc_v[...].astype(dp_v.dtype)[None]
    down_cp = [remote(dp_v.at[ffn], dp_v.at[ffn], ffn_peer(d)) for d in range(1, n_ffn)]
    for j, (c0, cw) in enumerate(chunks):
        store(av[j], a_o.at[:, :, pl.ds(c0, cw)])
    for cp in dn2_cp:
        cp.wait_recv()
    loads["g2"].wait()
    loads["dxo"].wait()
    dn2 = dn2_v[0]
    for i in range(1, n_ffn):
        dn2 = dn2 + dn2_v[i]
    dn2_s[...] = dn2
    for cp in down_cp:
        cp.wait_recv()
    down = dp_v[0].astype(F32)
    for i in range(1, n_ffn):
        down = down + dp_v[i].astype(F32)
    x2 = (x_v[...].astype(F32) + down).astype(BF16).astype(F32)
    gdn = g2_v[...] * dn2_s[...]
    stat2[pl.ds(hid, 1)] = (column_to_row(jnp.sum(x2 * x2, axis=-1, keepdims=True), 0) + column_to_row(jnp.sum(gdn * x2, axis=-1, keepdims=True), tokens))[None]
    st2 = [remote(stat2.at[hid], stat2.at[hid], hid_peer(d)) for d in range(1, n_hid)]
    acc_v[...] = x2
    for cp in st2:
        cp.wait_recv()
    tot2 = jnp.sum(stat2[...], axis=0)
    r2 = lax.rsqrt(row_to_column(tot2, tokens, 0) / d_model + NORM_EPS)
    c2 = row_to_column(tot2, tokens, tokens)
    x2 = acc_v[...]
    e_val = dxo_v[...].astype(F32) + (r2 * (g2_v[...] * dn2_s[...]) - x2 * (r2 * r2 * r2) * (c2 / d_model))
    e_v[...] = e_val
    eb_v[...] = e_val.astype(BF16)

    d2d = []
    for j, (c0, cw) in enumerate(chunks):
        for hf in range(2):
            part2[j][hf] = dot_nt(eb_v[...], wd_v[hf * half + c0 : hf * half + c0 + cw, :])
        d2d.append(remote(part2[j].at[1 - core], rx2[j], {"hid": partner}))
    rs = []
    for j, (c0, cw) in enumerate(chunks):
        d2d[j].wait_recv()
        for b in range(chips):
            rows = slice(b * tb, (b + 1) * tb)
            sb2[j][b] = (part2[j][core, rows, :] + rx2[j][rows, :]).astype(sb2[j].dtype)
        rs.append([remote(sb2[j].at[(chip + d) % chips], rr2[j].at[d - 1], chip_peer(d)) for d in range(1, chips)])
    store(eb_v, eb_o)
    x2 = acc_v[...]
    n2_v[...] = (x2 * r2 * g2_v[...]).astype(BF16)
    store(n2_v, n2_o)
    dg2_o[...] = jnp.sum(dn2_s[...] * x2 * r2, axis=0, keepdims=True)
    ag = []
    for j, (c0, cw) in enumerate(chunks):
        for cp in rs[j]:
            cp.wait_recv()
        d_act = part2[j][core, my_rows, :] + rx2[j][my_rows, :]
        for d in range(chips - 1):
            d_act = d_act + rr2[j][d].astype(F32)
        dgu[j][core, 0, my_rows, :] = (d_act * pre[j][...]).astype(BF16)
        dgu[j][core, 1, my_rows, :] = (d_act * sil[j][...]).astype(BF16)
        ag.append([remote(dgu[j].at[core, :, my_rows], dgu[j].at[core, :, my_rows], chip_peer(d)) for d in range(1, chips)])
    relay = []
    for j, (c0, cw) in enumerate(chunks):
        for cp in ag[j]:
            cp.wait_recv()
        relay.append(remote(dgu[j].at[core], dgu[j].at[core], {"hid": partner}))
    for j, (c0, cw) in enumerate(chunks):
        relay[j].wait_recv()
        prod = None
        for hf in range(2):
            lo = hf * half + c0
            valid = min(cw, ffw - lo)
            for gu, w_v in enumerate((wg_v, wu_v)):
                term = dot_nt(dgu[j][hf, gu, :, 0:valid], w_v[:, lo : lo + valid])
                prod = term if prod is None else prod + term
        acc_v[...] = prod if j == 0 else acc_v[...] + prod
    dn1p = acc_v[...]
    dn1_v[pl.ds(ffn, 1)] = dn1p.astype(dn1_v.dtype)[None]
    dn1_cp = [remote(dn1_v.at[ffn], dn1_v.at[ffn], ffn_peer(d)) for d in range(1, n_ffn)]
    me = ffn * n_hid + hid
    stat3[pl.ds(me, 1)] = column_to_row(jnp.sum(g1_v[...] * x_v[...].astype(F32) * dn1p, axis=-1, keepdims=True), 0)[None]
    pl.semaphore_wait(row_sem, n_ffn - 1)
    st3 = []
    for df in range(n_ffn):
        for d in range(n_hid):
            if df or d:
                st3.append(remote(stat3.at[me], stat3.at[me], {"ffn": (ffn + df) % n_ffn, "hid": (hid + d) % n_hid}))
    for j, (c0, cw) in enumerate(chunks):
        store(dgu[j], dgu_o.at[:, :, :, pl.ds(c0, cw)])
    for cp in dn1_cp:
        cp.wait_recv()
    dn1 = dn1_v[0].astype(F32)
    for i in range(1, n_ffn):
        dn1 = dn1 + dn1_v[i].astype(F32)
    x_f32 = x_v[...].astype(F32)
    dg1_o[...] = jnp.sum(dn1 * x_f32 * r1, axis=0, keepdims=True)
    for cp in st3:
        cp.wait_recv()
    c1 = row_to_column(jnp.sum(stat3[...], axis=0), tokens, 0)
    d_in = r1 * (g1_v[...] * dn1) - x_f32 * (r1 * r1 * r1) * (c1 / d_model)
    dx_o[...] = (e_v[...] + d_in).astype(BF16)
    for cp in sent:
        cp.wait_send()
    for cp in outs:
        cp.wait()


def weight_kernel(cfg, n1_r, n2_r, eb_r, a_r, dgu_r, dq_r, dwg_o, dwu_o, dwd_o, dwq_o, wg_s, wu_s, wd_s, wq_s, sem):
    tokens, width, ffw, qw = cfg["tokens"], cfg["width"], cfg["ffw"], cfg["qw"]
    half = half_width(ffw)
    rb = 128
    copies = []

    def flush(src, dst):
        cp = pltpu.make_async_copy(src, dst, sem.at[len(copies)])
        cp.start()
        copies.append(cp)

    for r0 in range(0, width, rb):
        rows = pl.ds(r0, rb)
        n2_t = n2_r[:, r0 : r0 + rb].T
        wq_s[rows, :] = dot_nn(n2_t, dq_r[...]).astype(BF16)
        flush(wq_s.at[rows], dwq_o.at[rows])
    for r0 in range(0, ffw, 2 * rb):
        size = min(2 * rb, ffw - r0)
        cuts = sorted({r0, min(max(half, r0), r0 + size), r0 + size})
        for lo, hi in zip(cuts[:-1], cuts[1:]):
            hf = lo // half
            wd_s[lo:hi, :] = dot_tn(a_r[hf, :, lo - hf * half : hi - hf * half], eb_r[...]).astype(BF16)
        rows = pl.ds(r0, size)
        flush(wd_s.at[rows], dwd_o.at[rows])
    for r0 in range(0, width, rb):
        rows = pl.ds(r0, rb)
        n1_t = n1_r[:, r0 : r0 + rb].T
        for gu, (s_r, o_r) in enumerate(((wg_s, dwg_o), (wu_s, dwu_o))):
            s_r[rows, 0:half] = dot_nn(n1_t, dgu_r[0, gu]).astype(BF16)
            s_r[rows, half:ffw] = dot_nn(n1_t, dgu_r[1, gu, :, 0 : ffw - half]).astype(BF16)
            flush(s_r.at[rows], o_r.at[rows])
    for cp in copies:
        cp.wait()


def solution(mesh):
    n_hid, n_ffn = mesh.shape["hid"], mesh.shape["ffn"]

    def local_step(x_in, gain_one, gain_two, w_gate, w_up, w_down, w_qkv, dx_out, d_qkv):
        tokens, width = x_in.shape
        ffw, qw = w_gate.shape[1], w_qkv.shape[1]
        half = half_width(ffw)
        chunks = chunk_list(half)
        chips = n_hid // 2
        tb = tokens // chips
        cfg = dict(n_hid=n_hid, n_ffn=n_ffn, tokens=tokens, width=width, ffw=ffw, qw=qw)
        vm = pltpu.VMEM
        per = lambda shape, dt: [vm(shape(cw), dt) for _, cw in chunks]
        scratch = [
            vm((tokens, width), BF16), vm((1, width), F32), vm((1, width), F32),
            vm((width, ffw), BF16), vm((width, ffw), BF16), vm((2 * half, width), BF16), vm((width, qw), BF16),
            vm((tokens, width), BF16), vm((tokens, qw), BF16),
            vm((tokens, width), BF16), vm((tokens, width), BF16), vm((tokens, width), BF16), vm((tokens, width), F32),
            vm((n_ffn, tokens, width), F32),
            vm((n_hid, 1, LANES), F32), vm((n_hid, 1, LANES), F32), vm((n_hid * n_ffn, 1, LANES), F32),
            vm((n_ffn, tokens, width), BF16), vm((n_ffn, tokens, width), BF16), vm((tokens, width), F32), vm((tokens, width), F32),
        ]
        scratch += per(lambda cw: (2, 2, tokens, cw), F32)
        scratch += per(lambda cw: (2, tokens, cw), F32)
        scratch += per(lambda cw: (chips, 2, tb, cw), BF16)
        scratch += per(lambda cw: (chips - 1, 2, tb, cw), BF16)
        scratch += per(lambda cw: (2, tokens, cw), BF16)
        scratch += per(lambda cw: (tb, cw), F32)
        scratch += per(lambda cw: (tb, cw), F32)
        scratch += per(lambda cw: (2, tokens, cw), F32)
        scratch += per(lambda cw: (tokens, cw), F32)
        scratch += per(lambda cw: (chips, tb, cw), BF16)
        scratch += per(lambda cw: (chips - 1, tb, cw), BF16)
        scratch += per(lambda cw: (2, 2, tokens, cw), BF16)
        n_copy = 2 * (n_hid - 1) + 3 * (n_ffn - 1) + len(chunks) * (4 + 4 * (chips - 1)) + n_hid * n_ffn - 1
        n_out = 3 + 2 * len(chunks)
        scratch += [pltpu.SemaphoreType.DMA((9,)), pltpu.SemaphoreType.DMA((n_out,)), pltpu.SemaphoreType.DMA((n_copy,)), pltpu.SemaphoreType.DMA((n_copy,)), pltpu.SemaphoreType.REGULAR]
        any_spec = pl.BlockSpec(memory_space=pl.ANY)
        vm_spec = pl.BlockSpec(memory_space=pltpu.VMEM)
        sds = jax.ShapeDtypeStruct
        dx_in, dg1, dg2, n1, n2, eb, a_full, dgu_full = pl.pallas_call(
            functools.partial(chain_kernel, cfg),
            out_shape=(
                sds((tokens, width), BF16), sds((1, width), F32), sds((1, width), F32),
                sds((tokens, width), BF16), sds((tokens, width), BF16), sds((tokens, width), BF16),
                sds((2, tokens, half), BF16), sds((2, 2, tokens, half), BF16),
            ),
            in_specs=[any_spec] * 9,
            out_specs=(vm_spec,) * 3 + (any_spec,) * 5,
            scratch_shapes=scratch,
            compiler_params=pltpu.CompilerParams(collective_id=0, has_side_effects=True, vmem_limit_bytes=VMEM_LIMIT),
            name="chain",
        )(x_in, gain_one.reshape(1, width), gain_two.reshape(1, width), w_gate, w_up, w_down, w_qkv, dx_out, d_qkv)
        n_flush = 3 * (width // 128) + -(-ffw // 256)
        dwg, dwu, dwd, dwq = pl.pallas_call(
            functools.partial(weight_kernel, cfg),
            out_shape=(sds((width, ffw), BF16), sds((width, ffw), BF16), sds((ffw, width), BF16), sds((width, qw), BF16)),
            in_specs=[vm_spec] * 6,
            out_specs=(any_spec,) * 4,
            scratch_shapes=[vm((width, ffw), BF16), vm((width, ffw), BF16), vm((ffw, width), BF16), vm((width, qw), BF16), pltpu.SemaphoreType.DMA((n_flush,))],
            compiler_params=pltpu.CompilerParams(vmem_limit_bytes=VMEM_LIMIT),
            name="weights",
        )(n1, n2, eb, a_full, dgu_full, d_qkv)
        return dx_in, dwg, dwu, dwd, dwq, dg1.reshape(width), dg2.reshape(width)

    tok_spec = P("data", "hid")
    in_specs = (tok_spec, P("hid"), P("hid"), P("hid", "ffn"), P("hid", "ffn"), P("ffn", "hid"), P("hid", "ffn"), tok_spec, P("data", "ffn"))
    out_specs = (tok_spec, P(("data", "hid"), "ffn"), P(("data", "hid"), "ffn"), P(("data", "ffn"), "hid"), P(("data", "hid"), "ffn"), P(("data", "hid")), P(("data", "hid")))
    return jax.shard_map(local_step, mesh=mesh, in_specs=in_specs, out_specs=out_specs, check_vma=False)
```

time: 284 us -> 79.1 us (0.28)
  waiting for transfers between devices: 171 us -> 0 us
  Pallas kernels: 0 us -> 61.4 us
  blocking collectives: 55.4 us -> 0 us
  matrix products: 29.2 us -> 0 us
  local copies, waits for them, and re-layouts: 1.5 us -> 16.8 us
  between operations: 13.9 us -> 0.68 us
  other arithmetic: 11.5 us -> 0 us
    psum x4 -> x0, waiting for transfers between devices: 171 us -> none  [the longest x1 56.4 us: local_step(): gate_pre, up_pre = lax.psum((gate_part, up_part), 'hid')]
    pallas_call x0 -> x2, Pallas kernels: none -> 61.4 us  [the longest x1 55.1 us: local_step(): pl.pallas_call(functools.partial(chain_kernel, cfg), out_shape=(sds((toke...]
    psum x4 -> x0, blocking collectives: 55.4 us -> none  [the longest x2 28.5 us: norm_forward(): inv_rms = lax.rsqrt(lax.psum(sq_part, 'hid') / d_model + NORM_EPS)]
    dot_general x11 -> x0, matrix products: 29.2 us -> none  [the longest x4 12.3 us: dot_tn(): lax.dot_general(a_mat, b_mat, (((0,), (0,)), ((), ())), preferred_element...]
    unnamed x22 -> x17, local copies, waits for them, and re-layouts: 1.5 us -> 16.8 us
    reduce_sum x4 -> x0, other arithmetic: 5.28 us -> none  [the longest x2 3.15 us: norm_backward(): d_gain = jnp.sum(d_norm * z_val * inv_rms, axis=0)]
    convert_element_type x3 -> x0, other arithmetic: 5.22 us -> none  [the longest x1 2.03 us: local_step(): d_up = (d_act * gate_silu).astype(jnp.bfloat16)]
  transfers between devices with their start and end apart: 4 -> 0, of which waited for: 4 -> 0; matrix products, arithmetic and copies ran while one was open for 4% -> 0% of each run, Pallas kernels for 0% -> 0%
where the time goes in v1:
time: 79.1 us; the launch traced here: 78.9 us
  Pallas kernels  61.4 us (78%)
  local copies, waits for them, and re-layouts  16.8 us (21%)
    pallas_call x1, Pallas kernels, local_step(): pl.pallas_call(functools.partial(chain_kernel, cfg), out_shape=(sds((toke...  55.1 us
    unnamed x17, local copies, waits for them, and re-layouts  16.8 us
    pallas_call x1, Pallas kernels, local_step(): pl.pallas_call(functools.partial(weight_kernel, cfg), out_shape=(sds((wid...  6.33 us

profile of v1, /device:TPU:97, one launch (start us, length us, event | category | flops | bytes accessed | tf_op | source)
XLA Modules:
  0.0 78.9 jit_solution(17680013657219138434)
XLA Ops:
  0.6 0.0 copy-start.1
  0.6 4.7 %copy.16.refs_3_ = bf16[512,2752]{1,0:T(8,128)(2,1)} copy(bf16[512,2752]{0,1:T(8,128)(2,1)} %param.12) | data formatting | bytes 5636096 | tf_op args[3]
  5.3 0.0 copy-done.1
  5.3 2.9 %copy.17.refs_4_ = bf16[512,2752]{1,0:T(8,128)(2,1)} copy(bf16[512,2752]{0,1:T(8,128)(2,1)S(1)} %copy-done.1) | data formatting | bytes 5636096 | tf_op args[4]
  8.3 55.1 %chain.1 = (bf16[64,512]{1,0:T(8,128)(2,1)}, f32[1,512]{1,0:T(1,128)}, f32[1,512]{1,0:T(1,128)}, bf16[64,512]{1,0:T(8,128)(2,1)}, bf16[64,512]{1,0:T(8,128)(2,1)...) custom-call(bf16[64,512]{1,0:T(8,128)(2,1)} %refs_0_.1, ...), custom_call_target="tpu_custom_call" | custom-call | tf_op jit(solution)/shard_map/chain/pallas_call | solution.py:392
  63.4 6.3 %weights.1 = (bf16[512,2752]{1,0:T(8,128)(2,1)}, bf16[512,2752]{1,0:T(8,128)(2,1)}, bf16[2752,512]{1,0:T(8,128)(2,1)}, bf16[512,3072]{1,0:T(8,128)(2,1)}) custom-call(bf16[64,512]{1,0:T(8,128)(2,1)} %get-tuple-element.20.n1_r, bf16[64,512]{1,0:T(8,128)(2,1)} %get-tuple-element.21.n2_r, bf16[64,512]{1,0:T(8,128)(2,1)} %get-tuple-element.22.eb_r, ...), custom_call_target="tpu_custom_call" | custom-call | tf_op jit(solution)/shard_map/weights/pallas_call | solution.py:406
  69.7 0.0 copy-start
  69.7 4.7 %copy.18 = bf16[512,2752]{0,1:T(8,128)(2,1)} copy(bf16[512,2752]{1,0:T(8,128)(2,1)} %get-tuple-element.32) | data formatting | bytes 5636096
  74.4 0.0 copy-done
  74.4 0.0 copy-start.2
  74.4 0.0 copy-start.4
  74.4 0.0 copy-start.3
  74.4 2.7 %copy.19 = bf16[512,2752]{0,1:T(8,128)(2,1)} copy(bf16[512,2752]{1,0:T(8,128)(2,1)S(1)} %copy-done) | data formatting | bytes 5636096
  77.1 0.0 copy-done.2
  77.1 0.6 copy.23
  77.8 0.0 copy-done.4
  77.8 0.6 copy.24
  78.3 0.0 copy-done.3
  78.3 0.6 copy.25
Async XLA Ops:
  0.6 4.7 %copy-start.1 = (bf16[512,2752]{0,1:T(8,128)(2,1)S(1)}, bf16[512,2752]{0,1:T(8,128)(2,1)}, u32[]{:S(2)}) copy-start(bf16[512,2752]{0,1:T(8,128)(2,1)} %param.13) | copy-start | bytes 8454148
  69.7 4.7 %copy-start = (bf16[512,2752]{1,0:T(8,128)(2,1)S(1)}, bf16[512,2752]{1,0:T(8,128)(2,1)}, u32[]{:S(2)}) copy-start(bf16[512,2752]{1,0:T(8,128)(2,1)} %get-tuple-element.33) | copy-start | bytes 8454148
  74.4 2.7 %copy-start.2 = (bf16[64,512]{1,0:T(8,128)(2,1)S(1)}, bf16[64,512]{1,0:T(8,128)(2,1)}, u32[]{:S(2)}) copy-start(bf16[64,512]{1,0:T(8,128)(2,1)} %get-tuple-element.45) | copy-start | bytes 196612
  74.4 3.3 %copy-start.4 = (f32[1,512]{1,0:T(1,128)S(1)}, f32[1,512]{1,0:T(1,128)}, u32[]{:S(2)}) copy-start(f32[1,512]{1,0:T(1,128)} %get-tuple-element.29) | copy-start | bytes 6148
  74.4 3.9 %copy-start.3 = (f32[1,512]{1,0:T(1,128)S(1)}, f32[1,512]{1,0:T(1,128)}, u32[]{:S(2)}) copy-start(f32[1,512]{1,0:T(1,128)} %get-tuple-element.30) | copy-start | bytes 6148

commit v2 on v1

--- a/solution.py
+++ b/solution.py
@@ -13,7 +13,9 @@
 MESH = pl.DeviceIdType.MESH
 VMEM_LIMIT = 60 * 1024 * 1024
 LANES = 128
-CHUNK = 512
+CHUNK = 384
+ROW_BLOCK = 256
+QKV_BLOCK = 128
 
 
 def dot_nn(a_mat, b_mat):
@@ -33,9 +35,11 @@
 
 
 def chunk_list(half):
+    tiles = half // LANES
+    n = -(-tiles * LANES // CHUNK)
+    sizes = [(tiles // n + (i >= n - tiles % n)) * LANES for i in range(n)]
     out, at = [], 0
-    while at < half:
-        size = min(CHUNK, half - at)
+    for size in sizes:
         out.append((at, size))
         at += size
     return out
@@ -66,7 +70,7 @@
     x_h, g1_h, g2_h, wg_h, wu_h, wd_h, wq_h, dxo_h, dq_h = [next(it) for _ in range(9)]
     dx_o, dg1_o, dg2_o, n1_o, n2_o, eb_o, a_o, dgu_o = [next(it) for _ in range(8)]
     x_v, g1_v, g2_v, wg_v, wu_v, wd_v, wq_v, dxo_v, dq_v = [next(it) for _ in range(9)]
-    n1_v, n2_v, eb_v, e_v, dn2_v, stat1, stat2, stat3, dp_v, dn1_v, acc_v, dn2_s = [next(it) for _ in range(12)]
+    n1_v, n2_v, eb_v, e_v, dn2_v, stat1, stat2, stat3, dp_v, dn1_v, acc_v, dn2_s, acc2_v, x2_v = [next(it) for _ in range(14)]
     part = [next(it) for _ in range(nj)]
     rx = [next(it) for _ in range(nj)]
     sb = [next(it) for _ in range(nj)]
@@ -119,8 +123,8 @@
     load("g1", g1_h, g1_v)
     load("dq", dq_h, dq_v)
     load("wq", wq_h, wq_v)
-    load("wg", wg_h, wg_v)
-    load("wu", wu_h, wu_v)
+    load("wg", wg_h, wg_v.at[pl.ds(0, ffw)])
+    load("wu", wu_h, wu_v.at[pl.ds(0, ffw)])
     load("wd", wd_h, wd_v.at[pl.ds(0, ffw)])
     load("g2", g2_h, g2_v)
     load("dxo", dxo_h, dxo_v)
@@ -139,7 +143,8 @@
         pl.semaphore_signal(barrier, inc=1, device_id=ffn_peer(d), device_id_type=MESH)
 
     if 2 * half > ffw:
-        wd_v[pl.ds(ffw, 2 * half - ffw), :] = jnp.zeros((2 * half - ffw, width), BF16)
+        for w_v in (wg_v, wu_v, wd_v):
+            w_v[pl.ds(ffw, 2 * half - ffw), :] = jnp.zeros((2 * half - ffw, width), BF16)
 
     loads["x"].wait()
     x_f32 = x_v[...].astype(F32)
@@ -169,11 +174,8 @@
     for j, (c0, cw) in enumerate(chunks):
         for hf in range(2):
             lo = hf * half + c0
-            valid = min(cw, ffw - lo)
             for gu, w_v in enumerate((wg_v, wu_v)):
-                part[j][hf, gu, :, 0:valid] = dot_nn(n1_v[...], w_v[:, lo : lo + valid])
-                if valid < cw:
-                    part[j][hf, gu, :, valid:cw] = jnp.zeros((tokens, cw - valid), F32)
+                part[j][hf, gu] = dot_nt(n1_v[...], w_v[lo : lo + cw, :])
         d2d.append(remote(part[j].at[1 - core], rx[j], {"hid": partner}))
     rs = []
     for j, (c0, cw) in enumerate(chunks):
@@ -209,8 +211,13 @@
         relay[j].wait_recv()
         w_rows = pl.ds(pl.multiple_of((1 - core) * half, LANES) + c0, cw)
         acc_v[...] += dot_nn(av[j][1 - core], wd_v[w_rows, :])
-    dp_v[pl.ds(ffn, 1)] = acc_v[...].astype(dp_v.dtype)[None]
-    down_cp = [remote(dp_v.at[ffn], dp_v.at[ffn], ffn_peer(d)) for d in range(1, n_ffn)]
+    tf = tokens // n_ffn
+    f_rows = pl.ds(pl.multiple_of(ffn * tf, tf), tf)
+    down_cp = []
+    for d in range(1, n_ffn):
+        to = (ffn + d) % n_ffn
+        down_cp.append(remote(acc_v.at[pl.ds(pl.multiple_of(to * tf, tf), tf)], dp_v.at[ffn], {"ffn": to}))
+    dp_v[pl.ds(ffn, 1)] = acc_v[f_rows, :][None]
     for j, (c0, cw) in enumerate(chunks):
         store(av[j], a_o.at[:, :, pl.ds(c0, cw)])
     for cp in dn2_cp:
@@ -221,22 +228,38 @@
     for i in range(1, n_ffn):
         dn2 = dn2 + dn2_v[i]
     dn2_s[...] = dn2
+    pl.semaphore_wait(row_sem, n_ffn - 1)
+    me = ffn * n_hid + hid
+
+    def to_all(buf):
+        cps = []
+        for df in range(n_ffn):
+            for d in range(n_hid):
+                if df or d:
+                    cps.append(remote(buf.at[me], buf.at[me], {"ffn": (ffn + df) % n_ffn, "hid": (hid + d) % n_hid}))
+        return cps
+
     for cp in down_cp:
         cp.wait_recv()
-    down = dp_v[0].astype(F32)
-    for i in range(1, n_ffn):
-        down = down + dp_v[i].astype(F32)
-    x2 = (x_v[...].astype(F32) + down).astype(BF16).astype(F32)
-    gdn = g2_v[...] * dn2_s[...]
-    stat2[pl.ds(hid, 1)] = (column_to_row(jnp.sum(x2 * x2, axis=-1, keepdims=True), 0) + column_to_row(jnp.sum(gdn * x2, axis=-1, keepdims=True), tokens))[None]
-    st2 = [remote(stat2.at[hid], stat2.at[hid], hid_peer(d)) for d in range(1, n_hid)]
-    acc_v[...] = x2
+    x2 = (x_v[f_rows, :].astype(F32) + jnp.sum(dp_v[...], axis=0)).astype(BF16)
+    x2_v[f_rows, :] = x2
+    x2_cp = [remote(x2_v.at[f_rows], x2_v.at[f_rows], ffn_peer(d)) for d in range(1, n_ffn)]
+    x2 = x2.astype(F32)
+    gdn = g2_v[...] * dn2_s[f_rows, :]
+    stat2[pl.ds(me, 1)] = (column_to_row(jnp.sum(x2 * x2, axis=-1, keepdims=True), 0) + column_to_row(jnp.sum(gdn * x2, axis=-1, keepdims=True), tf))[None]
+    st2 = to_all(stat2)
+    for cp in x2_cp:
+        cp.wait_recv()
     for cp in st2:
         cp.wait_recv()
-    tot2 = jnp.sum(stat2[...], axis=0)
-    r2 = lax.rsqrt(row_to_column(tot2, tokens, 0) / d_model + NORM_EPS)
-    c2 = row_to_column(tot2, tokens, tokens)
-    x2 = acc_v[...]
+    ssq2, c2 = [], []
+    for i in range(n_ffn):
+        tot2 = jnp.sum(stat2[i * n_hid : (i + 1) * n_hid], axis=0)
+        ssq2.append(row_to_column(tot2, tf, 0))
+        c2.append(row_to_column(tot2, tf, tf))
+    ssq2, c2 = jnp.concatenate(ssq2, axis=0), jnp.concatenate(c2, axis=0)
+    r2 = lax.rsqrt(ssq2 / d_model + NORM_EPS)
+    x2 = x2_v[...].astype(F32)
     e_val = dxo_v[...].astype(F32) + (r2 * (g2_v[...] * dn2_s[...]) - x2 * (r2 * r2 * r2) * (c2 / d_model))
     e_v[...] = e_val
     eb_v[...] = e_val.astype(BF16)
@@ -254,7 +277,7 @@
             sb2[j][b] = (part2[j][core, rows, :] + rx2[j][rows, :]).astype(sb2[j].dtype)
         rs.append([remote(sb2[j].at[(chip + d) % chips], rr2[j].at[d - 1], chip_peer(d)) for d in range(1, chips)])
     store(eb_v, eb_o)
-    x2 = acc_v[...]
+    x2 = x2_v[...].astype(F32)
     n2_v[...] = (x2 * r2 * g2_v[...]).astype(BF16)
     store(n2_v, n2_o)
     dg2_o[...] = jnp.sum(dn2_s[...] * x2 * r2, axis=0, keepdims=True)
@@ -278,22 +301,15 @@
         prod = None
         for hf in range(2):
             lo = hf * half + c0
-            valid = min(cw, ffw - lo)
             for gu, w_v in enumerate((wg_v, wu_v)):
-                term = dot_nt(dgu[j][hf, gu, :, 0:valid], w_v[:, lo : lo + valid])
+                term = dot_nn(dgu[j][hf, gu], w_v[lo : lo + cw, :])
                 prod = term if prod is None else prod + term
-        acc_v[...] = prod if j == 0 else acc_v[...] + prod
-    dn1p = acc_v[...]
+        acc2_v[...] = prod if j == 0 else acc2_v[...] + prod
+    dn1p = acc2_v[...]
     dn1_v[pl.ds(ffn, 1)] = dn1p.astype(dn1_v.dtype)[None]
     dn1_cp = [remote(dn1_v.at[ffn], dn1_v.at[ffn], ffn_peer(d)) for d in range(1, n_ffn)]
-    me = ffn * n_hid + hid
     stat3[pl.ds(me, 1)] = column_to_row(jnp.sum(g1_v[...] * x_v[...].astype(F32) * dn1p, axis=-1, keepdims=True), 0)[None]
-    pl.semaphore_wait(row_sem, n_ffn - 1)
-    st3 = []
-    for df in range(n_ffn):
-        for d in range(n_hid):
-            if df or d:
-                st3.append(remote(stat3.at[me], stat3.at[me], {"ffn": (ffn + df) % n_ffn, "hid": (hid + d) % n_hid}))
+    st3 = to_all(stat3)
     for j, (c0, cw) in enumerate(chunks):
         store(dgu[j], dgu_o.at[:, :, :, pl.ds(c0, cw)])
     for cp in dn1_cp:
@@ -314,37 +330,48 @@
         cp.wait()
 
 
-def weight_kernel(cfg, n1_r, n2_r, eb_r, a_r, dgu_r, dq_r, dwg_o, dwu_o, dwd_o, dwq_o, wg_s, wu_s, wd_s, wq_s, sem):
+def weight_kernel(cfg, *refs):
     tokens, width, ffw, qw = cfg["tokens"], cfg["width"], cfg["ffw"], cfg["qw"]
     half = half_width(ffw)
-    rb = 128
+    it = iter(refs)
+    n1_h, n2_h, eb_h, a_h, dgu_h, dq_h, dx_r, dg1_r, dg2_r = [next(it) for _ in range(9)]
+    dx_o, dg1_o, dg2_o, dwg_o, dwu_o, dwd_o, dwq_o = [next(it) for _ in range(7)]
+    n1_r, n2_r, eb_r, a_r, dgu_r, dq_r, wg_s, wu_s, wd_s, wq_s, load_sem, sem = [next(it) for _ in range(12)]
     copies = []
+    loads = []
+    for i, (src, dst) in enumerate(((n2_h, n2_r), (dq_h, dq_r), (eb_h, eb_r), (a_h, a_r), (n1_h, n1_r), (dgu_h, dgu_r))):
+        loads.append(pltpu.make_async_copy(src, dst, load_sem.at[i]))
+        loads[-1].start()
 
     def flush(src, dst):
         cp = pltpu.make_async_copy(src, dst, sem.at[len(copies)])
         cp.start()
         copies.append(cp)
 
-    for r0 in range(0, width, rb):
-        rows = pl.ds(r0, rb)
-        n2_t = n2_r[:, r0 : r0 + rb].T
-        wq_s[rows, :] = dot_nn(n2_t, dq_r[...]).astype(BF16)
-        flush(wq_s.at[rows], dwq_o.at[rows])
-    for r0 in range(0, ffw, 2 * rb):
-        size = min(2 * rb, ffw - r0)
-        cuts = sorted({r0, min(max(half, r0), r0 + size), r0 + size})
-        for lo, hi in zip(cuts[:-1], cuts[1:]):
-            hf = lo // half
-            wd_s[lo:hi, :] = dot_tn(a_r[hf, :, lo - hf * half : hi - hf * half], eb_r[...]).astype(BF16)
-        rows = pl.ds(r0, size)
-        flush(wd_s.at[rows], dwd_o.at[rows])
-    for r0 in range(0, width, rb):
-        rows = pl.ds(r0, rb)
-        n1_t = n1_r[:, r0 : r0 + rb].T
-        for gu, (s_r, o_r) in enumerate(((wg_s, dwg_o), (wu_s, dwu_o))):
-            s_r[rows, 0:half] = dot_nn(n1_t, dgu_r[0, gu]).astype(BF16)
-            s_r[rows, half:ffw] = dot_nn(n1_t, dgu_r[1, gu, :, 0 : ffw - half]).astype(BF16)
-            flush(s_r.at[rows], o_r.at[rows])
+    def by_rows(lhs, rhs, out_s, out_o):
+        for r0 in range(0, ffw, ROW_BLOCK):
+            size = min(ROW_BLOCK, ffw - r0)
+            cuts = sorted({r0, min(max(half, r0), r0 + size), r0 + size})
+            for lo, hi in zip(cuts[:-1], cuts[1:]):
+                hf = lo // half
+                out_s[lo:hi, :] = dot_tn(lhs(hf, slice(lo - hf * half, hi - hf * half)), rhs[...]).astype(BF16)
+            flush(out_s.at[pl.ds(r0, size)], out_o.at[pl.ds(r0, size)])
+
+    dx_o[...] = dx_r[...]
+    dg1_o[...] = dg1_r[...]
+    dg2_o[...] = dg2_r[...]
+    for cp in loads[0:2]:
+        cp.wait()
+    for r0 in range(0, width, QKV_BLOCK):
+        wq_s[r0 : r0 + QKV_BLOCK, :] = dot_tn(n2_r[:, r0 : r0 + QKV_BLOCK], dq_r[...]).astype(BF16)
+        flush(wq_s.at[pl.ds(r0, QKV_BLOCK)], dwq_o.at[pl.ds(r0, QKV_BLOCK)])
+    for cp in loads[2:4]:
+        cp.wait()
+    by_rows(lambda hf, cols: a_r[hf, :, cols], eb_r, wd_s, dwd_o)
+    for cp in loads[4:6]:
+        cp.wait()
+    by_rows(lambda hf, cols: dgu_r[hf, 0, :, cols], n1_r, wg_s, dwg_o)
+    by_rows(lambda hf, cols: dgu_r[hf, 1, :, cols], n1_r, wu_s, dwu_o)
     for cp in copies:
         cp.wait()
 
@@ -364,12 +391,12 @@
         per = lambda shape, dt: [vm(shape(cw), dt) for _, cw in chunks]
         scratch = [
             vm((tokens, width), BF16), vm((1, width), F32), vm((1, width), F32),
-            vm((width, ffw), BF16), vm((width, ffw), BF16), vm((2 * half, width), BF16), vm((width, qw), BF16),
+            vm((2 * half, width), BF16), vm((2 * half, width), BF16), vm((2 * half, width), BF16), vm((width, qw), BF16),
             vm((tokens, width), BF16), vm((tokens, qw), BF16),
             vm((tokens, width), BF16), vm((tokens, width), BF16), vm((tokens, width), BF16), vm((tokens, width), F32),
             vm((n_ffn, tokens, width), F32),
-            vm((n_hid, 1, LANES), F32), vm((n_hid, 1, LANES), F32), vm((n_hid * n_ffn, 1, LANES), F32),
-            vm((n_ffn, tokens, width), BF16), vm((n_ffn, tokens, width), BF16), vm((tokens, width), F32), vm((tokens, width), F32),
+            vm((n_hid, 1, LANES), F32), vm((n_hid * n_ffn, 1, LANES), F32), vm((n_hid * n_ffn, 1, LANES), F32),
+            vm((n_ffn, tokens // n_ffn, width), F32), vm((n_ffn, tokens, width), BF16), vm((tokens, width), F32), vm((tokens, width), F32), vm((tokens, width), F32), vm((tokens, width), BF16),
         ]
         scratch += per(lambda cw: (2, 2, tokens, cw), F32)
         scratch += per(lambda cw: (2, tokens, cw), F32)
@@ -383,7 +410,7 @@
         scratch += per(lambda cw: (chips, tb, cw), BF16)
         scratch += per(lambda cw: (chips - 1, tb, cw), BF16)
         scratch += per(lambda cw: (2, 2, tokens, cw), BF16)
-        n_copy = 2 * (n_hid - 1) + 3 * (n_ffn - 1) + len(chunks) * (4 + 4 * (chips - 1)) + n_hid * n_ffn - 1
+        n_copy = n_hid - 1 + 4 * (n_ffn - 1) + len(chunks) * (4 + 4 * (chips - 1)) + 2 * (n_hid * n_ffn - 1)
         n_out = 3 + 2 * len(chunks)
         scratch += [pltpu.SemaphoreType.DMA((9,)), pltpu.SemaphoreType.DMA((n_out,)), pltpu.SemaphoreType.DMA((n_copy,)), pltpu.SemaphoreType.DMA((n_copy,)), pltpu.SemaphoreType.REGULAR]
         any_spec = pl.BlockSpec(memory_space=pl.ANY)
@@ -401,18 +428,26 @@
             scratch_shapes=scratch,
             compiler_params=pltpu.CompilerParams(collective_id=0, has_side_effects=True, vmem_limit_bytes=VMEM_LIMIT),
             name="chain",
-        )(x_in, gain_one.reshape(1, width), gain_two.reshape(1, width), w_gate, w_up, w_down, w_qkv, dx_out, d_qkv)
-        n_flush = 3 * (width // 128) + -(-ffw // 256)
-        dwg, dwu, dwd, dwq = pl.pallas_call(
+        )(x_in, gain_one.reshape(1, width), gain_two.reshape(1, width), w_gate.T, w_up.T, w_down, w_qkv, dx_out, d_qkv)
+        n_flush = width // QKV_BLOCK + 3 * -(-ffw // ROW_BLOCK)
+        dx_in, dg1, dg2, dwg, dwu, dwd, dwq = pl.pallas_call(
             functools.partial(weight_kernel, cfg),
-            out_shape=(sds((width, ffw), BF16), sds((width, ffw), BF16), sds((ffw, width), BF16), sds((width, qw), BF16)),
-            in_specs=[vm_spec] * 6,
-            out_specs=(any_spec,) * 4,
-            scratch_shapes=[vm((width, ffw), BF16), vm((width, ffw), BF16), vm((ffw, width), BF16), vm((width, qw), BF16), pltpu.SemaphoreType.DMA((n_flush,))],
+            out_shape=(
+                sds((tokens, width), BF16), sds((1, width), F32), sds((1, width), F32),
+                sds((ffw, width), BF16), sds((ffw, width), BF16), sds((ffw, width), BF16), sds((width, qw), BF16),
+            ),
+            in_specs=[any_spec] * 6 + [vm_spec] * 3,
+            out_specs=(vm_spec,) * 3 + (any_spec,) * 4,
+            scratch_shapes=[
+                vm((tokens, width), BF16), vm((tokens, width), BF16), vm((tokens, width), BF16),
+                vm((2, tokens, half), BF16), vm((2, 2, tokens, half), BF16), vm((tokens, qw), BF16),
+                vm((ffw, width), BF16), vm((ffw, width), BF16), vm((ffw, width), BF16), vm((width, qw), BF16),
+                pltpu.SemaphoreType.DMA((6,)), pltpu.SemaphoreType.DMA((n_flush,)),
+            ],
             compiler_params=pltpu.CompilerParams(vmem_limit_bytes=VMEM_LIMIT),
             name="weights",
-        )(n1, n2, eb, a_full, dgu_full, d_qkv)
-        return dx_in, dwg, dwu, dwd, dwq, dg1.reshape(width), dg2.reshape(width)
+        )(n1, n2, eb, a_full, dgu_full, d_qkv, dx_in, dg1, dg2)
+        return dx_in, dwg.T, dwu.T, dwd, dwq, dg1.reshape(width), dg2.reshape(width)
 
     tok_spec = P("data", "hid")
     in_specs = (tok_spec, P("hid"), P("hid"), P("hid", "ffn"), P("hid", "ffn"), P("ffn", "hid"), P("hid", "ffn"), tok_spec, P("data", "ffn"))

time: 79.1 us -> 64.7 us (0.82)
  local copies, waits for them, and re-layouts: 16.8 us -> 0 us
  Pallas kernels: 61.4 us -> 63.9 us
    unnamed x17 -> x0, local copies, waits for them, and re-layouts: 16.8 us -> none
    pallas_call x1, Pallas kernels: 55.1 us -> 56.4 us  [local_step(): pl.pallas_call(functools.partial(chain_kernel, cfg), out_shape=(sds((toke...]
    pallas_call x1, Pallas kernels: 6.33 us -> 7.5 us  [local_step(): pl.pallas_call(functools.partial(weight_kernel, cfg), out_shape=(sds((tok...]
where the time goes in v2:
time: 64.7 us; the launch traced here: 64.5 us
  Pallas kernels  63.9 us (99%)
    pallas_call x1, Pallas kernels, local_step(): pl.pallas_call(functools.partial(chain_kernel, cfg), out_shape=(sds((toke...  56.4 us
    pallas_call x1, Pallas kernels, local_step(): pl.pallas_call(functools.partial(weight_kernel, cfg), out_shape=(sds((tok...  7.5 us

profile of v2, /device:TPU:97, one launch (start us, length us, event | category | flops | bytes accessed | tf_op | source)
XLA Modules:
  0.0 64.5 jit_solution(2940484510083565476)
XLA Ops:
  0.6 56.4 %chain.1 = (bf16[64,512]{1,0:T(8,128)(2,1)}, f32[1,512]{1,0:T(1,128)}, f32[1,512]{1,0:T(1,128)}, bf16[64,512]{1,0:T(8,128)(2,1)}, bf16[64,512]{1,0:T(8,128)(2,1)...) custom-call(bf16[64,512]{1,0:T(8,128)(2,1)} %refs_0_.1, ...), custom_call_target="tpu_custom_call" | custom-call | tf_op jit(solution)/shard_map/chain/pallas_call | solution.py:419
  57.0 7.5 %weights.1 = (bf16[64,512]{1,0:T(8,128)(2,1)}, f32[1,512]{1,0:T(1,128)}, f32[1,512]{1,0:T(1,128)}, bf16[2752,512]{1,0:T(8,128)(2,1)}, bf16[2752,512]{1,0:T(8,128...) custom-call(bf16[64,512]{1,0:T(8,128)(2,1)} %get-tuple-element.22.refs_0_, ...), custom_call_target="tpu_custom_call" | custom-call | tf_op jit(solution)/shard_map/weights/pallas_call | solution.py:433

commit v3 on v2

--- a/solution.py
+++ b/solution.py
@@ -11,10 +11,11 @@
 F32 = jnp.float32
 BF16 = jnp.bfloat16
 MESH = pl.DeviceIdType.MESH
-VMEM_LIMIT = 60 * 1024 * 1024
+VMEM_LIMIT = 55_300_000
+FLUSH_LIMIT = 2 * 1024 * 1024
+FLUSH_PARTS = 4
 LANES = 128
 CHUNK = 384
-ROW_BLOCK = 256
 QKV_BLOCK = 128
 
 
@@ -43,6 +44,10 @@
         out.append((at, size))
         at += size
     return out
+
+
+def far_first(n):
+    return sorted(range(1, n), key=lambda d: -min(d, n - d))
 
 
 def column_to_row(col, shift):
@@ -68,7 +73,7 @@
     d_model = width * n_hid
     it = iter(refs)
     x_h, g1_h, g2_h, wg_h, wu_h, wd_h, wq_h, dxo_h, dq_h = [next(it) for _ in range(9)]
-    dx_o, dg1_o, dg2_o, n1_o, n2_o, eb_o, a_o, dgu_o = [next(it) for _ in range(8)]
+    dx_o, dg1_o, dg2_o, dwg_o, dwu_o, dwd_o, dwq_o = [next(it) for _ in range(7)]
     x_v, g1_v, g2_v, wg_v, wu_v, wd_v, wq_v, dxo_v, dq_v = [next(it) for _ in range(9)]
     n1_v, n2_v, eb_v, e_v, dn2_v, stat1, stat2, stat3, dp_v, dn1_v, acc_v, dn2_s, acc2_v, x2_v = [next(it) for _ in range(14)]
     part = [next(it) for _ in range(nj)]
@@ -83,7 +88,7 @@
     sb2 = [next(it) for _ in range(nj)]
     rr2 = [next(it) for _ in range(nj)]
     dgu = [next(it) for _ in range(nj)]
-    load_sem, out_sem, send_sem, recv_sem, row_sem = [next(it) for _ in range(5)]
+    load_sem, send_sem, recv_sem, row_sem = [next(it) for _ in range(4)]
 
     hid = lax.axis_index("hid")
     ffn = lax.axis_index("ffn")
@@ -129,12 +134,12 @@
     load("g2", g2_h, g2_v)
     load("dxo", dxo_h, dxo_v)
 
-    outs = []
-
-    def store(src, dst):
-        cp = pltpu.make_async_copy(src, dst, out_sem.at[len(outs)])
-        cp.start()
-        outs.append(cp)
+    def by_rows(lhs, rhs, out):
+        for hf in range(2):
+            for j, (c0, cw) in enumerate(chunks):
+                lo = hf * half + c0
+                size = min(cw, ffw - lo)
+                out[lo : lo + size, :] = dot_tn(lhs(j, hf)[:, 0:size], rhs[...]).astype(BF16)
 
     barrier = pltpu.get_barrier_semaphore()
     for d in range(1, n_hid):
@@ -151,14 +156,14 @@
     stat1[pl.ds(hid, 1)] = column_to_row(jnp.sum(x_f32 * x_f32, axis=-1, keepdims=True), 0)[None]
 
     pl.semaphore_wait(barrier, n_hid - 1 + n_ffn - 1)
-    st1 = [remote(stat1.at[hid], stat1.at[hid], hid_peer(d)) for d in range(1, n_hid)]
+    st1 = [remote(stat1.at[hid], stat1.at[hid], hid_peer(d)) for d in far_first(n_hid)]
     for d in range(1, n_ffn):
         pl.semaphore_signal(row_sem, inc=1, device_id=ffn_peer(d), device_id_type=MESH)
 
     loads["dq"].wait()
     loads["wq"].wait()
     dn2_v[pl.ds(ffn, 1)] = dot_nt(dq_v[...], wq_v[...])[None]
-    dn2_cp = [remote(dn2_v.at[ffn], dn2_v.at[ffn], ffn_peer(d)) for d in range(1, n_ffn)]
+    dn2_cp = [remote(dn2_v.at[ffn], dn2_v.at[ffn], ffn_peer(d)) for d in far_first(n_ffn)]
 
     loads["g1"].wait()
     for cp in st1:
@@ -166,7 +171,6 @@
     ssq1 = row_to_column(jnp.sum(stat1[...], axis=0), tokens, 0)
     r1 = lax.rsqrt(ssq1 / d_model + NORM_EPS)
     n1_v[...] = (x_v[...].astype(F32) * r1 * g1_v[...]).astype(BF16)
-    store(n1_v, n1_o)
 
     loads["wg"].wait()
     loads["wu"].wait()
@@ -183,7 +187,7 @@
         for b in range(chips):
             rows = slice(b * tb, (b + 1) * tb)
             sb[j][b] = (part[j][core, :, rows, :] + rx[j][:, rows, :]).astype(sb[j].dtype)
-        rs.append([remote(sb[j].at[(chip + d) % chips], rr[j].at[d - 1], chip_peer(d)) for d in range(1, chips)])
+        rs.append([remote(sb[j].at[(chip + d) % chips], rr[j].at[d - 1], chip_peer(d)) for d in far_first(chips)])
     ag = []
     for j, (c0, cw) in enumerate(chunks):
         for cp in rs[j]:
@@ -195,7 +199,7 @@
         sig = jax.nn.sigmoid(gate)
         silu = gate * sig
         av[j][core, my_rows, :] = (silu * up).astype(BF16)
-        ag.append([remote(av[j].at[core, my_rows], av[j].at[core, my_rows], chip_peer(d)) for d in range(1, chips)])
+        ag.append([remote(av[j].at[core, my_rows], av[j].at[core, my_rows], chip_peer(d)) for d in far_first(chips)])
         sil[j][...] = silu
         pre[j][...] = up * sig * (1.0 + gate * (1.0 - sig))
     loads["wd"].wait()
@@ -218,8 +222,6 @@
         to = (ffn + d) % n_ffn
         down_cp.append(remote(acc_v.at[pl.ds(pl.multiple_of(to * tf, tf), tf)], dp_v.at[ffn], {"ffn": to}))
     dp_v[pl.ds(ffn, 1)] = acc_v[f_rows, :][None]
-    for j, (c0, cw) in enumerate(chunks):
-        store(av[j], a_o.at[:, :, pl.ds(c0, cw)])
     for cp in dn2_cp:
         cp.wait_recv()
     loads["g2"].wait()
@@ -232,18 +234,21 @@
     me = ffn * n_hid + hid
 
     def to_all(buf):
+        far = lambda d, n: min(d, n - d)
+        hops = sorted(((df, dc) for df in range(n_ffn) for dc in range(chips)), key=lambda p: -far(p[0], n_ffn) - far(p[1], chips))
         cps = []
-        for df in range(n_ffn):
-            for d in range(n_hid):
-                if df or d:
-                    cps.append(remote(buf.at[me], buf.at[me], {"ffn": (ffn + df) % n_ffn, "hid": (hid + d) % n_hid}))
+        for df, dc in hops:
+            for flip in range(2):
+                if df or dc or flip:
+                    to_hid = (chip + dc) % chips * 2 + (1 - core if flip else core)
+                    cps.append(remote(buf.at[me], buf.at[me], {"ffn": (ffn + df) % n_ffn, "hid": to_hid}))
         return cps
 
     for cp in down_cp:
         cp.wait_recv()
     x2 = (x_v[f_rows, :].astype(F32) + jnp.sum(dp_v[...], axis=0)).astype(BF16)
     x2_v[f_rows, :] = x2
-    x2_cp = [remote(x2_v.at[f_rows], x2_v.at[f_rows], ffn_peer(d)) for d in range(1, n_ffn)]
+    x2_cp = [remote(x2_v.at[f_rows], x2_v.at[f_rows], ffn_peer(d)) for d in far_first(n_ffn)]
     x2 = x2.astype(F32)
     gdn = g2_v[...] * dn2_s[f_rows, :]
     stat2[pl.ds(me, 1)] = (column_to_row(jnp.sum(x2 * x2, axis=-1, keepdims=True), 0) + column_to_row(jnp.sum(gdn * x2, axis=-1, keepdims=True), tf))[None]
@@ -275,11 +280,11 @@
         for b in range(chips):
             rows = slice(b * tb, (b + 1) * tb)
             sb2[j][b] = (part2[j][core, rows, :] + rx2[j][rows, :]).astype(sb2[j].dtype)
-        rs.append([remote(sb2[j].at[(chip + d) % chips], rr2[j].at[d - 1], chip_peer(d)) for d in range(1, chips)])
-    store(eb_v, eb_o)
+        rs.append([remote(sb2[j].at[(chip + d) % chips], rr2[j].at[d - 1], chip_peer(d)) for d in far_first(chips)])
     x2 = x2_v[...].astype(F32)
     n2_v[...] = (x2 * r2 * g2_v[...]).astype(BF16)
-    store(n2_v, n2_o)
+    for r0 in range(0, width, QKV_BLOCK):
+        dwq_o[r0 : r0 + QKV_BLOCK, :] = dot_tn(n2_v[:, r0 : r0 + QKV_BLOCK], dq_v[...]).astype(BF16)
     dg2_o[...] = jnp.sum(dn2_s[...] * x2 * r2, axis=0, keepdims=True)
     ag = []
     for j, (c0, cw) in enumerate(chunks):
@@ -290,7 +295,8 @@
             d_act = d_act + rr2[j][d].astype(F32)
         dgu[j][core, 0, my_rows, :] = (d_act * pre[j][...]).astype(BF16)
         dgu[j][core, 1, my_rows, :] = (d_act * sil[j][...]).astype(BF16)
-        ag.append([remote(dgu[j].at[core, :, my_rows], dgu[j].at[core, :, my_rows], chip_peer(d)) for d in range(1, chips)])
+        ag.append([remote(dgu[j].at[core, :, my_rows], dgu[j].at[core, :, my_rows], chip_peer(d)) for d in far_first(chips)])
+    by_rows(lambda j, hf: av[j][hf], eb_v, dwd_o)
     relay = []
     for j, (c0, cw) in enumerate(chunks):
         for cp in ag[j]:
@@ -307,11 +313,11 @@
         acc2_v[...] = prod if j == 0 else acc2_v[...] + prod
     dn1p = acc2_v[...]
     dn1_v[pl.ds(ffn, 1)] = dn1p.astype(dn1_v.dtype)[None]
-    dn1_cp = [remote(dn1_v.at[ffn], dn1_v.at[ffn], ffn_peer(d)) for d in range(1, n_ffn)]
+    dn1_cp = [remote(dn1_v.at[ffn], dn1_v.at[ffn], ffn_peer(d)) for d in far_first(n_ffn)]
     stat3[pl.ds(me, 1)] = column_to_row(jnp.sum(g1_v[...] * x_v[...].astype(F32) * dn1p, axis=-1, keepdims=True), 0)[None]
     st3 = to_all(stat3)
-    for j, (c0, cw) in enumerate(chunks):
-        store(dgu[j], dgu_o.at[:, :, :, pl.ds(c0, cw)])
+    by_rows(lambda j, hf: dgu[j][hf, 0], n1_v, dwg_o)
+    by_rows(lambda j, hf: dgu[j][hf, 1], n1_v, dwu_o)
     for cp in dn1_cp:
         cp.wait_recv()
     dn1 = dn1_v[0].astype(F32)
@@ -326,52 +332,21 @@
     dx_o[...] = (e_v[...] + d_in).astype(BF16)
     for cp in sent:
         cp.wait_send()
-    for cp in outs:
-        cp.wait()
-
-
-def weight_kernel(cfg, *refs):
-    tokens, width, ffw, qw = cfg["tokens"], cfg["width"], cfg["ffw"], cfg["qw"]
-    half = half_width(ffw)
-    it = iter(refs)
-    n1_h, n2_h, eb_h, a_h, dgu_h, dq_h, dx_r, dg1_r, dg2_r = [next(it) for _ in range(9)]
-    dx_o, dg1_o, dg2_o, dwg_o, dwu_o, dwd_o, dwq_o = [next(it) for _ in range(7)]
-    n1_r, n2_r, eb_r, a_r, dgu_r, dq_r, wg_s, wu_s, wd_s, wq_s, load_sem, sem = [next(it) for _ in range(12)]
+
+
+def flush_pieces(shape):
+    rows = shape[0] // FLUSH_PARTS if shape[0] % (16 * FLUSH_PARTS) == 0 else shape[0]
+    return [pl.ds(r0, rows) for r0 in range(0, shape[0], rows)]
+
+
+def flush_kernel(*refs):
+    n_out = len(refs) // 2
+    sem = refs[-1]
     copies = []
-    loads = []
-    for i, (src, dst) in enumerate(((n2_h, n2_r), (dq_h, dq_r), (eb_h, eb_r), (a_h, a_r), (n1_h, n1_r), (dgu_h, dgu_r))):
-        loads.append(pltpu.make_async_copy(src, dst, load_sem.at[i]))
-        loads[-1].start()
-
-    def flush(src, dst):
-        cp = pltpu.make_async_copy(src, dst, sem.at[len(copies)])
-        cp.start()
-        copies.append(cp)
-
-    def by_rows(lhs, rhs, out_s, out_o):
-        for r0 in range(0, ffw, ROW_BLOCK):
-            size = min(ROW_BLOCK, ffw - r0)
-            cuts = sorted({r0, min(max(half, r0), r0 + size), r0 + size})
-            for lo, hi in zip(cuts[:-1], cuts[1:]):
-                hf = lo // half
-                out_s[lo:hi, :] = dot_tn(lhs(hf, slice(lo - hf * half, hi - hf * half)), rhs[...]).astype(BF16)
-            flush(out_s.at[pl.ds(r0, size)], out_o.at[pl.ds(r0, size)])
-
-    dx_o[...] = dx_r[...]
-    dg1_o[...] = dg1_r[...]
-    dg2_o[...] = dg2_r[...]
-    for cp in loads[0:2]:
-        cp.wait()
-    for r0 in range(0, width, QKV_BLOCK):
-        wq_s[r0 : r0 + QKV_BLOCK, :] = dot_tn(n2_r[:, r0 : r0 + QKV_BLOCK], dq_r[...]).astype(BF16)
-        flush(wq_s.at[pl.ds(r0, QKV_BLOCK)], dwq_o.at[pl.ds(r0, QKV_BLOCK)])
-    for cp in loads[2:4]:
-        cp.wait()
-    by_rows(lambda hf, cols: a_r[hf, :, cols], eb_r, wd_s, dwd_o)
-    for cp in loads[4:6]:
-        cp.wait()
-    by_rows(lambda hf, cols: dgu_r[hf, 0, :, cols], n1_r, wg_s, dwg_o)
-    by_rows(lambda hf, cols: dgu_r[hf, 1, :, cols], n1_r, wu_s, dwu_o)
+    for src, dst in zip(refs[:n_out], refs[n_out : 2 * n_out]):
+        for rows in flush_pieces(src.shape):
+            copies.append(pltpu.make_async_copy(src.at[rows], dst.at[rows], sem.at[len(copies)]))
+            copies[-1].start()
     for cp in copies:
         cp.wait()
 
@@ -411,42 +386,32 @@
         scratch += per(lambda cw: (chips - 1, tb, cw), BF16)
         scratch += per(lambda cw: (2, 2, tokens, cw), BF16)
         n_copy = n_hid - 1 + 4 * (n_ffn - 1) + len(chunks) * (4 + 4 * (chips - 1)) + 2 * (n_hid * n_ffn - 1)
-        n_out = 3 + 2 * len(chunks)
-        scratch += [pltpu.SemaphoreType.DMA((9,)), pltpu.SemaphoreType.DMA((n_out,)), pltpu.SemaphoreType.DMA((n_copy,)), pltpu.SemaphoreType.DMA((n_copy,)), pltpu.SemaphoreType.REGULAR]
-        any_spec = pl.BlockSpec(memory_space=pl.ANY)
+        scratch += [pltpu.SemaphoreType.DMA((9,)), pltpu.SemaphoreType.DMA((n_copy,)), pltpu.SemaphoreType.DMA((n_copy,)), pltpu.SemaphoreType.REGULAR]
+        any_spec = pl.BlockSpec(memory_space=pltpu.HBM)
         vm_spec = pl.BlockSpec(memory_space=pltpu.VMEM)
         sds = jax.ShapeDtypeStruct
-        dx_in, dg1, dg2, n1, n2, eb, a_full, dgu_full = pl.pallas_call(
+        results = (
+            ((tokens, width), BF16), ((1, width), F32), ((1, width), F32),
+            ((ffw, width), BF16), ((ffw, width), BF16), ((ffw, width), BF16), ((width, qw), BF16),
+        )
+        outs = pl.pallas_call(
             functools.partial(chain_kernel, cfg),
-            out_shape=(
-                sds((tokens, width), BF16), sds((1, width), F32), sds((1, width), F32),
-                sds((tokens, width), BF16), sds((tokens, width), BF16), sds((tokens, width), BF16),
-                sds((2, tokens, half), BF16), sds((2, 2, tokens, half), BF16),
-            ),
+            out_shape=tuple(vm(shape, dt) for shape, dt in results),
             in_specs=[any_spec] * 9,
-            out_specs=(vm_spec,) * 3 + (any_spec,) * 5,
+            out_specs=(vm_spec,) * 7,
             scratch_shapes=scratch,
             compiler_params=pltpu.CompilerParams(collective_id=0, has_side_effects=True, vmem_limit_bytes=VMEM_LIMIT),
             name="chain",
         )(x_in, gain_one.reshape(1, width), gain_two.reshape(1, width), w_gate.T, w_up.T, w_down, w_qkv, dx_out, d_qkv)
-        n_flush = width // QKV_BLOCK + 3 * -(-ffw // ROW_BLOCK)
         dx_in, dg1, dg2, dwg, dwu, dwd, dwq = pl.pallas_call(
-            functools.partial(weight_kernel, cfg),
-            out_shape=(
-                sds((tokens, width), BF16), sds((1, width), F32), sds((1, width), F32),
-                sds((ffw, width), BF16), sds((ffw, width), BF16), sds((ffw, width), BF16), sds((width, qw), BF16),
-            ),
-            in_specs=[any_spec] * 6 + [vm_spec] * 3,
-            out_specs=(vm_spec,) * 3 + (any_spec,) * 4,
-            scratch_shapes=[
-                vm((tokens, width), BF16), vm((tokens, width), BF16), vm((tokens, width), BF16),
-                vm((2, tokens, half), BF16), vm((2, 2, tokens, half), BF16), vm((tokens, qw), BF16),
-                vm((ffw, width), BF16), vm((ffw, width), BF16), vm((ffw, width), BF16), vm((width, qw), BF16),
-                pltpu.SemaphoreType.DMA((6,)), pltpu.SemaphoreType.DMA((n_flush,)),
-            ],
-            compiler_params=pltpu.CompilerParams(vmem_limit_bytes=VMEM_LIMIT),
-            name="weights",
-        )(n1, n2, eb, a_full, dgu_full, d_qkv, dx_in, dg1, dg2)
+            flush_kernel,
+            out_shape=tuple(sds(shape, dt) for shape, dt in results),
+            in_specs=[vm_spec] * 7,
+            out_specs=(any_spec,) * 7,
+            scratch_shapes=[pltpu.SemaphoreType.DMA((sum(len(flush_pieces(shape)) for shape, _ in results),))],
+            compiler_params=pltpu.CompilerParams(vmem_limit_bytes=FLUSH_LIMIT),
+            name="flush",
+        )(*outs)
         return dx_in, dwg.T, dwu.T, dwd, dwq, dg1.reshape(width), dg2.reshape(width)
 
     tok_spec = P("data", "hid")

time: 64.7 us -> 59.9 us (0.926)
  Pallas kernels: 63.9 us -> 59.1 us
    pallas_call x2, Pallas kernels: 63.9 us -> 59.1 us  [the longest x1 54.7 us: local_step(): pl.pallas_call(functools.partial(chain_kernel, cfg), out_shape=tuple((vm(...]
where the time goes in v3:
time: 59.9 us; the launch traced here: 59.8 us
  Pallas kernels  59.1 us (99%)
  between operations  0.64 us (1%)
    pallas_call x1, Pallas kernels, local_step(): pl.pallas_call(functools.partial(chain_kernel, cfg), out_shape=tuple((vm(...  54.7 us
    pallas_call x1, Pallas kernels, local_step(): pl.pallas_call(flush_kernel, out_shape=tuple((sds(shape, dt) for shape, d...  4.48 us

profile of v3, /device:TPU:97, one launch (start us, length us, event | category | flops | bytes accessed | tf_op | source)
XLA Modules:
  0.0 59.8 jit_solution(13396005474236522501)
XLA Ops:
  0.6 54.7 %chain.1 = (bf16[64,512]{1,0:T(8,128)(2,1)S(1)}, f32[1,512]{1,0:T(1,128)S(1)}, f32[1,512]{1,0:T(1,128)S(1)}, bf16[2752,512]{1,0:T(8,128)(2,1)S(1)}, bf16[2752,51...) custom-call(bf16[64,512]{1,0:T(8,128)(2,1)} %refs_0_.1, f32[1,512]{1,0:T(1,128)} %bitcast.10, ...), custom_call_target="tpu_custom_call" | custom-call | tf_op jit(solution)/shard_map/chain/pallas_call | solution.py:397
  55.3 4.5 %flush.1 = (bf16[64,512]{1,0:T(8,128)(2,1)}, f32[1,512]{1,0:T(1,128)}, f32[1,512]{1,0:T(1,128)}, bf16[2752,512]{1,0:T(8,128)(2,1)}, bf16[2752,512]{1,0:T(8,128)(...) custom-call(bf16[64,512]{1,0:T(8,128)(2,1)S(1)} %get-tuple-element.21.refs_0_, ...), custom_call_target="tpu_custom_call" | custom-call | tf_op jit(solution)/shard_map/flush/pallas_call | solution.py:406
